TPU v7x, 32 devices: a whole 2x2x4 slice. The times are simulated.
32 devices in a mesh: cols: 4 (over y, x), dom: 8 (over z, core).
Axes of the slice: x: 2, y: 2, z: 4, core: 2. Of those that a mesh axis runs over, the one named last changes fastest.
Arguments:
- features: bfloat16 [768, 4096], P('cols', 'dom'), may hold values from -6 to 6
- proj_in: bfloat16 [768, 256], P('cols'), may hold values from -0.3125 to 0.3125
- self_weight: bfloat16 [256, 256], replicated, may hold values from -0.375 to 0.375
- neigh_weight: bfloat16 [256, 256], replicated, may hold values from -0.375 to 0.375
- neighbors: int32 [16, 4096], P(None, 'dom'), may hold values from 0 to 1023, as said below
- degree: int32 [4096], P('dom'), may hold values from 1 to 16
- send_rows: int32 [8, 512], P('dom'), may hold values from 0 to 511
- send_count: int32 [8, 8], P('dom'), may hold values from 0 to 64, as said below
Outputs:
- layer_out: bfloat16 [256, 4096], P('cols', 'dom')
Inputs may be any that keep to these rules, and one draw needn't show every extreme that they name: `neighbors`: A code at or above 512 names a source partition other than the node's own and a slot below send_count of that source towards the node's partition. Every partition's rows are received in full (64 slots) from every other partition for at least one partition in every draw. `send_count`: zero on the diagonal; elsewhere 1 to 64, and 64 from every source towards at least one partition.
All inputs are finite; a program needn't handle non-finite values.
Results may differ from a plain program's by a relative error of at most 0.0051.
Values may be sent and summed in bfloat16 or wider, within the bound.
A program may use at most 64 MiB of HBM per device.

v0:
```python
import math

import jax
import jax.numpy as jnp
from jax import lax
from jax.sharding import PartitionSpec as P


def lead_dot(left, right):
    return lax.dot_general(
        left, right, (((0,), (0,)), ((), ())), preferred_element_type=jnp.float32
    )


def local(features, proj_in, self_weight, neigh_weight, neighbors, degree, send_rows, send_count):
    partial_value = lead_dot(proj_in, features)
    hidden = lax.psum_scatter(partial_value, "cols", scatter_dimension=0, tiled=True).astype(
        jnp.bfloat16
    )
    width = hidden.shape[0]
    nodes_here = hidden.shape[1]
    parts = lax.axis_size("dom")
    slots = send_rows.shape[1]
    capacity = slots // parts
    lane = jnp.arange(slots, dtype=jnp.int32)
    live = lane % capacity < send_count[0][lane // capacity]
    send_block = math.gcd(slots, 1024)
    send_groups = slots // send_block
    node_iota = jnp.arange(nodes_here, dtype=jnp.int32)[:, None]

    def select_rows(inputs):
        wanted, alive = inputs
        onehot = jnp.logical_and(node_iota == wanted[None, :], alive[None, :]).astype(jnp.bfloat16)
        return jnp.dot(hidden, onehot, preferred_element_type=jnp.float32).astype(jnp.bfloat16)

    chosen = lax.map(
        select_rows,
        (send_rows[0].reshape(send_groups, send_block), live.reshape(send_groups, send_block)),
    )
    outgoing = jnp.transpose(chosen, (1, 0, 2)).reshape(width, slots)
    incoming = lax.all_to_all(outgoing, "dom", split_axis=1, concat_axis=1, tiled=True)
    table = jnp.concatenate([hidden, incoming], axis=1)
    table_rows = table.shape[1]
    slot_count = neighbors.shape[0]
    used = jnp.arange(slot_count, dtype=jnp.int32)[:, None] < degree[None, :]
    codes = jnp.where(used, neighbors, -1)
    node_block = math.gcd(nodes_here, 256)
    node_groups = nodes_here // node_block
    grouped = jnp.transpose(codes.reshape(slot_count, node_groups, node_block), (1, 0, 2))
    table_iota = jnp.arange(table_rows, dtype=jnp.int32)[:, None]

    def aggregate(block_codes):
        counts = jnp.zeros((table_rows, node_block), jnp.bfloat16)
        for slot in range(slot_count):
            counts = counts + (table_iota == block_codes[slot][None, :]).astype(jnp.bfloat16)
        return jnp.dot(table, counts, preferred_element_type=jnp.float32)

    summed = lax.map(aggregate, grouped)
    total = jnp.transpose(summed, (1, 0, 2)).reshape(width, nodes_here)
    mean = (total / degree[None, :].astype(jnp.float32)).astype(jnp.bfloat16)
    column = lax.axis_index("cols")
    self_cols = lax.dynamic_slice_in_dim(self_weight, column * width, width, 1)
    neigh_cols = lax.dynamic_slice_in_dim(neigh_weight, column * width, width, 1)
    carry = lead_dot(self_cols, lax.all_gather(hidden, "cols", axis=0, tiled=True))
    result = carry + lead_dot(neigh_cols, lax.all_gather(mean, "cols", axis=0, tiled=True))
    return jnp.maximum(result, 0.0).astype(jnp.bfloat16)


def solution(mesh):
    return jax.shard_map(
        local,
        mesh=mesh,
        in_specs=(
            P("cols", "dom"),
            P("cols", None),
            P(),
            P(),
            P(None, "dom"),
            P("dom"),
            P("dom", None),
            P("dom", None),
        ),
        out_specs=P("cols", "dom"),
        check_vma=False,
    )
```

profile of v0, /device:TPU:0, one launch (start us, length us, event | category | flops | bytes accessed | tf_op | source)
XLA Modules:
  0.0 80.1 jit_solution(1586973152520998341)
XLA Ops:
  6.5 0.9 %copy-done = bf16[192,512]{1,0:T(8,128)(2,1)S(1)} copy-done((bf16[192,512]{1,0:T(8,128)(2,1)S(1)}, bf16[192,512]{1,0:T(8,128)(2,1)}, u32[]{:S(2)}) %copy-start) | copy-done | bytes 196632
  7.5 1.9 %fusion.83 = f32[256,512]{1,0:T(8,128)} fusion(bf16[192,256]{1,0:T(8,128)(2,1)} %param.11, bf16[192,512]{1,0:T(8,128)(2,1)S(1)} %copy-done), kind=kOutput, calls=%fused_computation.119 | convolution fusion | flops 50331648 | bytes 819200 | tf_op jit(solution)/shard_map/dot_general | solution.py:10
  9.5 0.7 copy-done.5
  10.2 0.6 copy-done.3
  10.9 0.7 fusion.82
  11.5 4.4 %compare_select_fusion.1 = s32[512,1]{0,1:T(1,128)S(1)} fusion(s32[]{:T(128)} %bitcast.3, s32[]{:T(128)} %bitcast.4, s32[]{:T(128)} %bitcast.5, s32[]{:T(128)} %bitcast.6, s32[]{:T(128)} %bitcast.7, s32[]{:T(128)} %bitcast.9, s32[]{:T(128)} %bitcast.8), kind=kLoop, calls=%fused_computation.99 | loop fusion | flops 11776 | bytes 2076 | tf_op jit(solution)/shard_map/gather | solution.py:26
  15.9 0.7 fusion.76
  16.6 21.4 %reduce-scatter.2.cloned.1.call-done = f32[64,512]{1,0:T(8,128)} async-done(((f32[256,512]{1,0:T(8,128)}), f32[64,512]{1,0:T(8,128)}) %reduce-scatter.2.cloned.1.call-update) | async-done | bytes 131088 | tf_op jit(solution)/shard_map/reduce_scatter | solution.py:17
  38.0 0.9 %convert_element_type.67 = bf16[64,512]{1,0:T(8,128)(2,1)S(1)} convert(f32[64,512]{1,0:T(8,128)} %reduce-scatter.2.cloned.1.call-done) | non-fusion elementwise | flops 32768 | bytes 196608 | tf_op jit(solution)/shard_map/convert_element_type | solution.py:17
  38.9 9.2 %all_gather.6 = bf16[256,512]{1,0:T(8,128)(2,1)S(1)} all-gather(bf16[64,512]{1,0:T(8,128)(2,1)S(1)} %convert_element_type.67), channel_id=1, replica_groups=mesh['cols'=4,'dom'=8] {'cols'}, dimensions={0}, use_global_device_ids=true | all-gather | bytes 327680 | tf_op jit(solution)/shard_map/all_gather | solution.py:64
  48.2 0.3 convolution_convert_fusion
  48.5 0.1 all_to_all.8
  48.7 0.8 reshape.155
  49.5 4.6 %all-to-all-start = ((bf16[8,2,2048]{2,1,0:T(2,128)(2,1)}), bf16[8,2,2048]{2,1,0:T(2,128)(2,1)S(1)}, u32[]{:S(2)}, u32[]{:S(2)}) async-start(bf16[8,2,2048]{2,1,0:T(2,128)(2,1)} %reshape.155), calls=%async_computation.1 | async-start | bytes 131072 | tf_op jit(solution)/shard_map/all_to_all | solution.py:41
  54.1 0.3 fusion.73
  54.3 5.6 %all-to-all-done = bf16[8,2,2048]{2,1,0:T(2,128)(2,1)S(1)} async-done(((bf16[8,2,2048]{2,1,0:T(2,128)(2,1)}), bf16[8,2,2048]{2,1,0:T(2,128)(2,1)S(1)}, u32[]{:S(2)}, u32[]{:S(2)}) %all-to-all-start) | async-done | bytes 65568 | tf_op jit(solution)/shard_map/all_to_all | solution.py:41
  60.0 0.1 reshape.156
  60.1 0.1 copy.12
  60.2 0.1 all_to_all.10
  60.4 4.0 %while.16 = (s32[]{:T(128)}, f32[2,64,256]{2,1,0:T(8,128)S(1)}, s32[2,16,256]{2,0,1:T(2,128)S(1)}, bf16[64,1024]{1,0:T(8,128)(2,1)S(1)}, s32[]{:T(128)}, /*index...) while((s32[]{:T(128)}, f32[2,64,256]{2,1,0:T(8,128)S(1)}, ...), condition=%wide.region_2.3_spmd.clone.clone, body=%wide.region_1.2_spmd.clone.clone.sunk | while | flops 50331664 | bytes 246205 | solution.py:58
  60.5 1.9 %fusion.95 = f32[2,64,256]{2,1,0:T(8,128)S(1)} fusion(f32[2,64,256]{2,1,0:T(8,128)S(1)} %get-tuple-element.253, s32[]{:T(128)S(6)} %copy.38, bf16[64,1024]{1,0:T(8,128)(2,1)S(1)} %get-tuple-element.276, s32[256]{0:T(256)S(1)} %bitcast.134, s32[256]{0:T(256)S(1)} %bitcast.120, s32[256]{0:T(256)S(1)} %bitcast.121, s32[256]{0:T(256)S(1)} %bitcast.122, ...), kind=kOutput, calls=%fused_computation.18.clone.1 | convolution fusion | flops 50331648 | bytes 212996 | tf_op jit(solution)/shard_map/while/body/eval_jaxpr/dot_general | solution.py:56
  62.5 1.9 %fusion.95 = f32[2,64,256]{2,1,0:T(8,128)S(1)} fusion(f32[2,64,256]{2,1,0:T(8,128)S(1)} %get-tuple-element.253, s32[]{:T(128)S(6)} %copy.38, bf16[64,1024]{1,0:T(8,128)(2,1)S(1)} %get-tuple-element.276, s32[256]{0:T(256)S(1)} %bitcast.134, s32[256]{0:T(256)S(1)} %bitcast.120, s32[256]{0:T(256)S(1)} %bitcast.121, s32[256]{0:T(256)S(1)} %bitcast.122, ...), kind=kOutput, calls=%fused_computation.18.clone.1 | convolution fusion | flops 50331648 | bytes 212996 | tf_op jit(solution)/shard_map/while/body/eval_jaxpr/dot_general | solution.py:56
  64.5 7.9 %all_gather.7 = bf16[256,512]{1,0:T(8,128)(2,1)S(1)} all-gather(bf16[64,512]{1,0:T(8,128)(2,1)S(1)} %divide_convert_fusion), channel_id=1, replica_groups=mesh['cols'=4,'dom'=8] {'cols'}, dimensions={0}, use_global_device_ids=true | all-gather | bytes 327680 | tf_op jit(solution)/shard_map/all_gather | solution.py:65
  72.4 0.9 %fusion.67 = bf16[64,512]{1,0:T(8,128)(2,1)} fusion(f32[64,512]{1,0:T(8,128)S(1)} %fusion.73, bf16[256,512]{1,0:T(8,128)(2,1)S(1)} %all_gather.7, bf16[256,256]{1,0:T(8,128)(2,1)S(1)} %copy-done.1, s32[]{:T(128)S(6)} %select_n.37), kind=kOutput, calls=%fused_computation.84 | convolution fusion | flops 16875520 | bytes 524292 | tf_op jit(solution)/shard_map/dot_general | solution.py:10
  (24 shorter events, 0.4 us)
Async XLA Ops:
  6.5 0.9 %copy-start = (bf16[192,512]{1,0:T(8,128)(2,1)S(1)}, bf16[192,512]{1,0:T(8,128)(2,1)}, u32[]{:S(2)}) copy-start(bf16[192,512]{1,0:T(8,128)(2,1)} %param.10) | copy-start | bytes 589828
  6.5 31.5 %reduce-scatter.2.cloned.1.call-start = ((), (), s32[]{:S(2)}) async-start(), calls=%async_computation.2 | async-start | bytes 655360 | tf_op jit(solution)/shard_map/reduce_scatter | solution.py:17
  9.4 0.8 copy-start.2
  9.4 0.7 copy-start.5
  10.2 0.7 copy-start.3
  38.9 9.2 %copy-start.6 = (s32[1,512]{1,0:T(1,128)S(1)}, s32[1,512]{1,0:T(1,128)}, u32[]{:S(2)}) copy-start(s32[1,512]{1,0:T(1,128)} %param.16) | copy-start | bytes 6148
  48.7 5.4 %copy-start.4 = (bf16[256,256]{1,0:T(8,128)(2,1)S(1)}, bf16[256,256]{1,0:T(8,128)(2,1)}, u32[]{:S(2)}) copy-start(bf16[256,256]{1,0:T(8,128)(2,1)} %param.12) | copy-start | bytes 393220
  49.5 10.5 %all-to-all-start = ((bf16[8,2,2048]{2,1,0:T(2,128)(2,1)}), bf16[8,2,2048]{2,1,0:T(2,128)(2,1)S(1)}, u32[]{:S(2)}, u32[]{:S(2)}) async-start(bf16[8,2,2048]{2,1,0:T(2,128)(2,1)} %reshape.155), calls=%async_computation.1 | async-start | bytes 131072 | tf_op jit(solution)/shard_map/all_to_all | solution.py:41
  64.5 7.9 %copy-start.1 = (bf16[256,256]{1,0:T(8,128)(2,1)S(1)}, bf16[256,256]{1,0:T(8,128)(2,1)}, u32[]{:S(2)}) copy-start(bf16[256,256]{1,0:T(8,128)(2,1)} %param.13) | copy-start | bytes 393220
Sparse Core Ops, SparseCore 0:
  10.2 27.8 reduce-scatter.1
where the time goes:
time: 80.6 us; the launch traced here: 80.1 us
  waiting for transfers between devices  27.1 us (34%)
  blocking collectives  17.1 us (21%)
  between operations  13.6 us (17%)
  matrix products  7.24 us (9%)
  other arithmetic  6.03 us (7%)
  starting transfers between devices  4.59 us (6%)
  local copies, waits for them, and re-layouts  4.42 us (5%)
    reduce_scatter x1, waiting for transfers between devices, local(): lax.psum_scatter(partial_value, 'cols', scatter_dimension=0, tiled=True)  21.4 us
    all_gather x1, blocking collectives, local(): lax.all_gather(hidden, 'cols', axis=0, tiled=True)  9.23 us
    all_gather x1, blocking collectives, local(): lax.all_gather(mean, 'cols', axis=0, tiled=True)  7.9 us
    all_to_all x1, waiting for transfers between devices, local(): lax.all_to_all(outgoing, 'dom', split_axis=1, concat_axis=1, tiled=True)  5.65 us
    all_to_all x1, starting transfers between devices, local(): lax.all_to_all(outgoing, 'dom', split_axis=1, concat_axis=1, tiled=True)  4.59 us
    gather x2, other arithmetic, local(): live = lane % capacity < send_count[0][lane // capacity]  4.42 us
    dot_general x2, matrix products, aggregate(): return jnp.dot(table, counts, preferred_element_type=jnp.float32)  3.79 us
    unnamed x16, local copies, waits for them, and re-layouts  3.19 us
  transfers between devices with their start and end apart: 2, of which 2 were waited for; matrix products, arithmetic and copies ran while one was open for 8% of the time, Pallas kernels for 0%

commit v1 on v0

v1 whole, which is shorter than its diff:
```python
import functools
import math

import jax
import jax.numpy as jnp
from jax import lax
from jax.experimental import pallas as pl
from jax.experimental.pallas import tpu as pltpu
from jax.sharding import PartitionSpec as P

MESH = pl.DeviceIdType.MESH
LANES = 128


def dot(left, right, left_dim, right_dim):
    return lax.dot_general(
        left, right, (((left_dim,), (right_dim,)), ((), ())), preferred_element_type=jnp.float32
    )


def kernel(
    cols,
    parts,
    capacity,
    feat_hbm,
    proj_hbm,
    selfw_hbm,
    neighw_hbm,
    neigh_hbm,
    degree_hbm,
    rows_hbm,
    count_hbm,
    out_ref,
    feat,
    proj,
    selfw,
    neighw,
    neigh,
    degree,
    rows,
    count,
    own,
    outgoing_sum,
    incoming_sum,
    hidden_all,
    mean_all,
    pick,
    packed_out,
    packed_in,
    table,
    counts,
    in_sem,
    sum_send,
    sum_recv,
    row_send,
    row_recv,
    hid_send,
    hid_recv,
    mean_send,
    mean_recv,
):
    column = lax.axis_index("cols")
    part = lax.axis_index("dom")
    width = out_ref.shape[0]
    nodes = out_ref.shape[1]
    hid = width * cols
    slots = rows.shape[1]
    slot_count = neigh.shape[0]
    fold = LANES // capacity
    short = width // fold

    loads = [
        pltpu.make_async_copy(source, target, in_sem.at[i])
        for i, (source, target) in enumerate(
            (
                (feat_hbm, feat),
                (proj_hbm, proj),
                (rows_hbm, rows),
                (count_hbm, count),
                (neigh_hbm, neigh),
                (degree_hbm, degree),
                (selfw_hbm, selfw),
                (neighw_hbm, neighw),
            )
        )
    ]
    for load in loads:
        load.start()

    barrier = pltpu.get_barrier_semaphore()
    for step in range(1, cols):
        pl.semaphore_signal(
            barrier, inc=1, device_id=((column + step) % cols, part), device_id_type=MESH
        )

    def greet(step, carry):
        pl.semaphore_signal(
            barrier, inc=1, device_id=(column, (part + step) % parts), device_id_type=MESH
        )
        return carry

    lax.fori_loop(1, parts, greet, 0)

    loads[0].wait()
    loads[1].wait()
    partial_value = dot(proj[...], feat[...], 0, 0)
    own[...] = partial_value
    outgoing_sum[...] = partial_value.astype(outgoing_sum.dtype)
    pl.semaphore_wait(barrier, cols + parts - 2)

    def band(index):
        return pl.ds(pl.multiple_of(index * width, width), width)

    def to_column(source, target, send, recv, step):
        peer = (column + step) % cols
        return pltpu.make_async_remote_copy(
            src_ref=source,
            dst_ref=target,
            send_sem=send.at[step - 1],
            recv_sem=recv.at[step - 1],
            device_id=(peer, part),
            device_id_type=MESH,
        )

    sums = [
        to_column(
            outgoing_sum.at[band((column + step) % cols)],
            incoming_sum.at[step - 1],
            sum_send,
            sum_recv,
            step,
        )
        for step in range(1, cols)
    ]
    for copy in sums:
        copy.start()

    for load in loads[2:]:
        load.wait()
    group = min(slots, 512)
    spread = group * fold

    def choose(index, carry):
        start = pl.multiple_of(index * group, group)
        wanted = rows[:, pl.ds(start, group)]
        source = (
            lax.broadcasted_iota(jnp.int32, (parts, group), 1) + start
        ) // capacity == lax.broadcasted_iota(jnp.int32, (parts, group), 0)
        amount = dot(
            jnp.broadcast_to(count[...].astype(jnp.float32), (8, parts)).astype(jnp.bfloat16),
            source.astype(jnp.float32).astype(jnp.bfloat16),
            1,
            0,
        )[0:1, :]
        slot = (lax.broadcasted_iota(jnp.int32, (1, group), 1) % capacity).astype(jnp.float32)
        wanted = jnp.where(slot < amount, wanted, -1)
        pieces = []
        for block in range(group // capacity):
            piece = wanted[:, block * capacity : (block + 1) * capacity]
            pieces += [piece] * fold
        wide = jnp.concatenate(pieces, axis=1)
        hit = lax.broadcasted_iota(jnp.int32, (nodes, spread), 0) == wide
        pick[:, pl.ds(pl.multiple_of(index * spread, spread), spread)] = jnp.where(
            hit, 1.0, 0.0
        ).astype(jnp.bfloat16)
        return carry

    lax.fori_loop(0, slots // group, choose, 0)

    used = lax.broadcasted_iota(jnp.int32, (slot_count, nodes), 0) < degree[...]
    codes = jnp.where(used, neigh[...], -1)
    neigh[...] = codes
    depth = 256
    row_of = lax.broadcasted_iota(jnp.int32, (depth, LANES), 0).astype(jnp.float32).astype(jnp.bfloat16)
    one = jnp.ones((depth, LANES), jnp.bfloat16)
    zero = jnp.zeros((depth, LANES), jnp.bfloat16)

    def tally(index, carry):
        start = pl.multiple_of(index * depth, depth)
        for lane in range(nodes // LANES):
            there = slice(lane * LANES, (lane + 1) * LANES)
            near = jnp.clip(neigh[:, there] - start, -1, depth).astype(jnp.float32)
            total = zero
            for slot in range(slot_count):
                code = jnp.broadcast_to(near[slot : slot + 1, :], (16, LANES)).astype(jnp.bfloat16)
                code = jnp.concatenate([code] * (depth // 16), axis=0)
                total = total + jnp.where(row_of == code, one, zero)
            counts[pl.ds(start, depth), there] = total
        return carry

    lax.fori_loop(0, counts.shape[0] // depth, tally, 0)

    mine = (
        lax.broadcasted_iota(jnp.int32, (width, hid), 0) + column * width
        == lax.broadcasted_iota(jnp.int32, (width, hid), 1)
    )
    mine = jnp.where(mine, 1.0, 0.0).astype(jnp.bfloat16)
    self_rows = dot(mine, selfw[...], 1, 1).astype(jnp.bfloat16)
    neigh_rows = dot(mine, neighw[...], 1, 1).astype(jnp.bfloat16)

    total = own[band(column), :]
    for step in range(1, cols):
        sums[step - 1].wait_recv()
    for step in range(1, cols):
        total = total + incoming_sum[step - 1].astype(jnp.float32)
    hidden = total.astype(jnp.bfloat16)
    hidden_all[band(column), :] = hidden

    folded = lax.broadcasted_iota(jnp.int32, (short, spread), 1) % LANES // capacity

    def pack(index, carry):
        start = pl.multiple_of(index * spread, spread)
        chosen = dot(hidden_all[band(column), :], pick[:, pl.ds(start, spread)], 1, 0)
        tight = chosen[0:short, :]
        for piece in range(1, fold):
            tight = jnp.where(folded == piece, chosen[piece * short : (piece + 1) * short, :], tight)
        tight = tight.astype(jnp.bfloat16)
        for block in range(spread // LANES):
            packed_out[index * (spread // LANES) + block] = tight[:, block * LANES : (block + 1) * LANES]
        return carry

    lax.fori_loop(0, slots // group, pack, 0)

    def to_part(step):
        peer = (part + step) % parts
        return pltpu.make_async_remote_copy(
            src_ref=packed_out.at[peer],
            dst_ref=packed_in.at[part],
            send_sem=row_send.at[step],
            recv_sem=row_recv.at[step],
            device_id=(column, peer),
            device_id_type=MESH,
        )

    def send_rows(step, carry):
        to_part(step).start()
        return carry

    lax.fori_loop(1, parts, send_rows, 0)

    def share(buffer, send, recv):
        return [
            to_column(buffer.at[band(column)], buffer.at[band(column)], send, recv, step)
            for step in range(1, cols)
        ]

    hidden_copies = share(hidden_all, hid_send, hid_recv)
    for copy in hidden_copies:
        copy.start()

    packed_in[part] = jnp.zeros((short, LANES), jnp.bfloat16)
    local_sum = dot(hidden, counts[0:nodes, :], 1, 0)

    def arrive(step, carry):
        to_part(step).wait_recv()
        return carry

    lax.fori_loop(1, parts, arrive, 0)

    half = lax.broadcasted_iota(jnp.int32, (short, LANES), 1) // capacity

    def unpack(index, carry):
        for piece in range(fold):
            value = jnp.zeros((short, LANES), jnp.float32)
            for place in range(fold):
                block = packed_in[index * fold + place].astype(jnp.float32)
                shift = (place - piece) * capacity % LANES
                if shift:
                    block = pltpu.roll(block, shift, 1)
                value = jnp.where(half == place, block, value)
            table[piece * short : (piece + 1) * short, pl.ds(pl.multiple_of(index * LANES, LANES), LANES)] = (
                value.astype(jnp.bfloat16)
            )
        return carry

    lax.fori_loop(0, parts // fold, unpack, 0)
    summed = local_sum + dot(table[...], counts[nodes:, :], 1, 0)
    mean_all[band(column), :] = (summed / degree[...].astype(jnp.float32)).astype(jnp.bfloat16)
    mean_copies = share(mean_all, mean_send, mean_recv)
    for copy in mean_copies:
        copy.start()
    for copy in hidden_copies:
        copy.wait_recv()
    result = dot(self_rows, hidden_all[...], 1, 0)
    for copy in mean_copies:
        copy.wait_recv()
    result = result + dot(neigh_rows, mean_all[...], 1, 0)
    out_ref[...] = jnp.maximum(result, 0.0).astype(out_ref.dtype)

    for copy in sums + hidden_copies + mean_copies:
        copy.wait_send()

    def sent(step, carry):
        to_part(step).wait_send()
        return carry

    lax.fori_loop(1, parts, sent, 0)


def local(features, proj_in, self_weight, neigh_weight, neighbors, degree, send_rows, send_count):
    cols = lax.axis_size("cols")
    parts = lax.axis_size("dom")
    hid = proj_in.shape[1]
    width = hid // cols
    nodes = features.shape[1]
    slots = send_rows.shape[1]
    capacity = slots // parts
    fold = LANES // capacity
    short = width // fold
    degree = degree.reshape(1, nodes)
    arguments = (
        features,
        proj_in,
        self_weight,
        neigh_weight,
        neighbors,
        degree,
        send_rows,
        send_count,
    )
    bf16 = jnp.bfloat16
    copies = pltpu.SemaphoreType.DMA
    return pl.pallas_call(
        functools.partial(kernel, cols, parts, capacity),
        out_shape=jax.ShapeDtypeStruct((width, nodes), bf16),
        in_specs=[pl.BlockSpec(memory_space=pl.ANY)] * len(arguments),
        out_specs=pl.BlockSpec(memory_space=pltpu.VMEM),
        scratch_shapes=[pltpu.VMEM(a.shape, a.dtype) for a in arguments]
        + [
            pltpu.VMEM((hid, nodes), jnp.float32),
            pltpu.VMEM((hid, nodes), bf16),
            pltpu.VMEM((cols - 1, width, nodes), bf16),
            pltpu.VMEM((hid, nodes), bf16),
            pltpu.VMEM((hid, nodes), bf16),
            pltpu.VMEM((nodes, slots * fold), bf16),
            pltpu.VMEM((parts, short, LANES), bf16),
            pltpu.VMEM((parts, short, LANES), bf16),
            pltpu.VMEM((width, slots), bf16),
            pltpu.VMEM((nodes + slots, nodes), bf16),
            copies((len(arguments),)),
            copies((cols - 1,)),
            copies((cols - 1,)),
            copies((parts,)),
            copies((parts,)),
            copies((cols - 1,)),
            copies((cols - 1,)),
            copies((cols - 1,)),
            copies((cols - 1,)),
        ],
        compiler_params=pltpu.CompilerParams(
            collective_id=0, has_side_effects=True, vmem_limit_bytes=48 * 1024 * 1024
        ),
        name="layer",
    )(*arguments)


def solution(mesh):
    return jax.shard_map(
        local,
        mesh=mesh,
        in_specs=(
            P("cols", "dom"),
            P("cols", None),
            P(),
            P(),
            P(None, "dom"),
            P("dom"),
            P("dom", None),
            P("dom", None),
        ),
        out_specs=P("cols", "dom"),
        check_vma=False,
    )
```

time: 80.6 us -> 28.1 us (0.35)
  waiting for transfers between devices: 27.1 us -> 0 us
  Pallas kernels: 0 us -> 20.7 us
  blocking collectives: 17.1 us -> 0 us
  between operations: 13.6 us -> 0.02 us
  matrix products: 7.24 us -> 0 us
  other arithmetic: 6.03 us -> 0 us
  starting transfers between devices: 4.59 us -> 0 us
  local copies, waits for them, and re-layouts: 4.42 us -> 7.03 us
    reduce_scatter x1 -> x0, waiting for transfers between devices: 21.4 us -> none  [local(): lax.psum_scatter(partial_value, 'cols', scatter_dimension=0, tiled=True)]
    pallas_call x0 -> x1, Pallas kernels: none -> 20.7 us  [local(): pl.pallas_call(functools.partial(kernel, cols, parts, capacity), out_shap...]
    all_gather x2 -> x0, blocking collectives: 17.1 us -> none  [the longest x1 9.23 us: local(): lax.all_gather(hidden, 'cols', axis=0, tiled=True)]
    dot_general x6 -> x0, matrix products: 7.24 us -> none  [the longest x2 3.79 us: aggregate(): return jnp.dot(table, counts, preferred_element_type=jnp.float32)]
    all_to_all x1 -> x0, waiting for transfers between devices: 5.65 us -> none  [local(): lax.all_to_all(outgoing, 'dom', split_axis=1, concat_axis=1, tiled=True)]
    all_to_all x1 -> x0, starting transfers between devices: 4.59 us -> none  [local(): lax.all_to_all(outgoing, 'dom', split_axis=1, concat_axis=1, tiled=True)]
    gather x2 -> x0, other arithmetic: 4.42 us -> none  [local(): live = lane % capacity < send_count[0][lane // capacity]]
    unnamed x16 -> x17, local copies, waits for them, and re-layouts: 3.19 us -> 7.03 us
  transfers between devices with their start and end apart: 2 -> 0, of which waited for: 2 -> 0; matrix products, arithmetic and copies ran while one was open for 8% -> 0% of each run, Pallas kernels for 0% -> 0%
where the time goes in v1:
time: 28.1 us; the launch traced here: 27.8 us
  Pallas kernels  20.7 us (74%)
  local copies, waits for them, and re-layouts  7.03 us (25%)
    pallas_call x1, Pallas kernels, local(): pl.pallas_call(functools.partial(kernel, cols, parts, capacity), out_shap...  20.7 us
    unnamed x17, local copies, waits for them, and re-layouts  7.03 us

profile of v1, /device:TPU:0, one launch (start us, length us, event | category | flops | bytes accessed | tf_op | source)
XLA Modules:
  0.0 27.8 jit_solution(987357809687873729)
XLA Ops:
  0.0 0.0 copy-start.7
  0.0 0.7 %copy-done.7 = s32[1,8]{1,0:T(1,128)S(1)} copy-done((s32[1,8]{1,0:T(1,128)S(1)}, s32[1,8]{1,0:T(1,128)}, u32[]{:S(2)}) %copy-start.7) | copy-done | bytes 56
  0.7 0.0 copy-start
  0.7 0.9 %copy-done = bf16[192,512]{1,0:T(8,128)(2,1)S(1)} copy-done((bf16[192,512]{1,0:T(8,128)(2,1)S(1)}, bf16[192,512]{1,0:T(8,128)(2,1)}, u32[]{:S(2)}) %copy-start) | copy-done | bytes 196632
  1.6 0.0 copy-start.1
  1.6 0.9 %copy-done.1 = bf16[256,256]{1,0:T(8,128)(2,1)S(1)} copy-done((bf16[256,256]{1,0:T(8,128)(2,1)S(1)}, bf16[256,256]{1,0:T(8,128)(2,1)}, u32[]{:S(2)}) %copy-start.1) | copy-done | bytes 131096
  2.5 0.0 copy-start.2
  2.5 0.9 %copy-done.2 = bf16[256,256]{1,0:T(8,128)(2,1)S(1)} copy-done((bf16[256,256]{1,0:T(8,128)(2,1)S(1)}, bf16[256,256]{1,0:T(8,128)(2,1)}, u32[]{:S(2)}) %copy-start.2) | copy-done | bytes 131096
  3.4 0.0 copy-start.3
  3.4 0.9 %copy-done.3 = bf16[192,256]{1,0:T(8,128)(2,1)S(1)} copy-done((bf16[192,256]{1,0:T(8,128)(2,1)S(1)}, bf16[192,256]{1,0:T(8,128)(2,1)}, u32[]{:S(2)}) %copy-start.3) | copy-done | bytes 98328
  4.3 0.0 copy-start.4
  4.3 0.8 %copy-done.4 = s32[16,512]{1,0:T(8,128)S(1)} copy-done((s32[16,512]{1,0:T(8,128)S(1)}, s32[16,512]{1,0:T(8,128)}, u32[]{:S(2)}) %copy-start.4) | copy-done | bytes 32792
  5.0 0.0 copy-start.5
  5.0 0.7 %copy-done.5 = s32[512]{0:T(512)S(1)} copy-done((s32[512]{0:T(512)S(1)}, s32[512]{0:T(512)}, u32[]{:S(2)}) %copy-start.5) | copy-done | bytes 2072
  5.7 0.0 copy-start.6
  5.7 0.7 %copy-done.6 = s32[1,512]{1,0:T(1,128)S(1)} copy-done((s32[1,512]{1,0:T(1,128)S(1)}, s32[1,512]{1,0:T(1,128)}, u32[]{:S(2)}) %copy-start.6) | copy-done | bytes 2072
  6.4 20.7 %layer.1 = bf16[64,512]{1,0:T(8,128)(2,1)S(1)} custom-call(bf16[192,512]{1,0:T(8,128)(2,1)S(1)} %copy-done, bf16[192,256]{1,0:T(8,128)(2,1)S(1)} %copy-done.3, bf16[256,256]{1,0:T(8,128)(2,1)S(1)} %copy-done.1, bf16[256,256]{1,0:T(8,128)(2,1)S(1)} %copy-done.2, s32[16,512]{1,0:T(8,128)S(1)} %copy-done.4, s32[1,512]{1,0:T(1,128)S(1)} %bitcast.1, ...), custom_call_target="tpu_custom_call" | custom-call | tf_op jit(solution)/shard_map/layer/pallas_call | solution.py:323
  27.2 0.6 %copy.10 = bf16[64,512]{1,0:T(8,128)(2,1)} copy(bf16[64,512]{1,0:T(8,128)(2,1)S(1)} %layer.1) | data formatting | bytes 131072
Async XLA Ops:
  0.0 0.7 %copy-start.7 = (s32[1,8]{1,0:T(1,128)S(1)}, s32[1,8]{1,0:T(1,128)}, u32[]{:S(2)}) copy-start(s32[1,8]{1,0:T(1,128)} %count_hbm.1) | copy-start | bytes 100
  0.7 0.9 %copy-start = (bf16[192,512]{1,0:T(8,128)(2,1)S(1)}, bf16[192,512]{1,0:T(8,128)(2,1)}, u32[]{:S(2)}) copy-start(bf16[192,512]{1,0:T(8,128)(2,1)} %feat_hbm.1) | copy-start | bytes 589828
  1.6 0.9 %copy-start.1 = (bf16[256,256]{1,0:T(8,128)(2,1)S(1)}, bf16[256,256]{1,0:T(8,128)(2,1)}, u32[]{:S(2)}) copy-start(bf16[256,256]{1,0:T(8,128)(2,1)} %selfw_hbm.1) | copy-start | bytes 393220
  2.5 0.9 %copy-start.2 = (bf16[256,256]{1,0:T(8,128)(2,1)S(1)}, bf16[256,256]{1,0:T(8,128)(2,1)}, u32[]{:S(2)}) copy-start(bf16[256,256]{1,0:T(8,128)(2,1)} %neighw_hbm.1) | copy-start | bytes 393220
  3.4 0.9 %copy-start.3 = (bf16[192,256]{1,0:T(8,128)(2,1)S(1)}, bf16[192,256]{1,0:T(8,128)(2,1)}, u32[]{:S(2)}) copy-start(bf16[192,256]{1,0:T(8,128)(2,1)} %proj_hbm.1) | copy-start | bytes 294916
  4.3 0.8 %copy-start.4 = (s32[16,512]{1,0:T(8,128)S(1)}, s32[16,512]{1,0:T(8,128)}, u32[]{:S(2)}) copy-start(s32[16,512]{1,0:T(8,128)} %neigh_hbm.1) | copy-start | bytes 98308
  5.0 0.7 %copy-start.5 = (s32[512]{0:T(512)S(1)}, s32[512]{0:T(512)}, u32[]{:S(2)}) copy-start(s32[512]{0:T(512)} %param.13) | copy-start | bytes 6148
  5.7 0.7 %copy-start.6 = (s32[1,512]{1,0:T(1,128)S(1)}, s32[1,512]{1,0:T(1,128)}, u32[]{:S(2)}) copy-start(s32[1,512]{1,0:T(1,128)} %rows_hbm.1) | copy-start | bytes 6148

commit v2 on v1

--- a/solution.py
+++ b/solution.py
@@ -323,7 +323,7 @@
     return pl.pallas_call(
         functools.partial(kernel, cols, parts, capacity),
         out_shape=jax.ShapeDtypeStruct((width, nodes), bf16),
-        in_specs=[pl.BlockSpec(memory_space=pl.ANY)] * len(arguments),
+        in_specs=[pl.BlockSpec(memory_space=pltpu.HBM)] * len(arguments),
         out_specs=pl.BlockSpec(memory_space=pltpu.VMEM),
         scratch_shapes=[pltpu.VMEM(a.shape, a.dtype) for a in arguments]
         + [
@@ -348,7 +348,7 @@
             copies((cols - 1,)),
         ],
         compiler_params=pltpu.CompilerParams(
-            collective_id=0, has_side_effects=True, vmem_limit_bytes=48 * 1024 * 1024
+            collective_id=0, has_side_effects=True, vmem_limit_bytes=67043328
         ),
         name="layer",
     )(*arguments)

time: 28.1 us -> 22.3 us (0.79)
  local copies, waits for them, and re-layouts: 7.03 us -> 1.47 us
    unnamed x17 -> x1, local copies, waits for them, and re-layouts: 7.03 us -> 1.47 us
where the time goes in v2:
time: 22.3 us; the launch traced here: 22.1 us
  Pallas kernels  20.6 us (92%)
  local copies, waits for them, and re-layouts  1.47 us (7%)
    pallas_call x1, Pallas kernels, local(): pl.pallas_call(functools.partial(kernel, cols, parts, capacity), out_shap...  20.6 us
    unnamed x1, local copies, waits for them, and re-layouts  1.47 us

profile of v2, /device:TPU:0, one launch (start us, length us, event | category | flops | bytes accessed | tf_op | source)
XLA Modules:
  0.0 22.1 jit_solution(1054490766892522131)
XLA Ops:
  0.0 20.6 %layer.1 = bf16[64,512]{1,0:T(8,128)(2,1)} custom-call(bf16[192,512]{1,0:T(8,128)(2,1)} %feat_hbm.1, bf16[192,256]{1,0:T(8,128)(2,1)} %proj_hbm.1, bf16[256,256]{1,0:T(8,128)(2,1)} %selfw_hbm.1, bf16[256,256]{1,0:T(8,128)(2,1)} %neighw_hbm.1, s32[16,512]{1,0:T(8,128)} %neigh_hbm.1, s32[1,512]{1,0:T(1,128)} %bitcast.1, s32[1,512]{1,0:T(1,128)} %rows_hbm.1, ...), custom_call_target="tpu_custom_call" | custom-call | tf_op jit(solution)/shard_map/layer/pallas_call | solution.py:323
  20.6 1.5 %copy.10 = bf16[64,512]{1,0:T(8,128)(2,1)} copy(bf16[64,512]{1,0:T(8,128)(2,1)} %layer.1) | data formatting | bytes 131072

commit v3 on v2

--- a/solution.py
+++ b/solution.py
@@ -135,7 +135,7 @@
     for copy in sums:
         copy.start()
 
-    for load in loads[2:]:
+    for load in loads[2:6]:
         load.wait()
     group = min(slots, 512)
     spread = group * fold
@@ -188,15 +188,7 @@
             counts[pl.ds(start, depth), there] = total
         return carry
 
-    lax.fori_loop(0, counts.shape[0] // depth, tally, 0)
-
-    mine = (
-        lax.broadcasted_iota(jnp.int32, (width, hid), 0) + column * width
-        == lax.broadcasted_iota(jnp.int32, (width, hid), 1)
-    )
-    mine = jnp.where(mine, 1.0, 0.0).astype(jnp.bfloat16)
-    self_rows = dot(mine, selfw[...], 1, 1).astype(jnp.bfloat16)
-    neigh_rows = dot(mine, neighw[...], 1, 1).astype(jnp.bfloat16)
+    lax.fori_loop(0, nodes // depth, tally, 0)
 
     total = own[band(column), :]
     for step in range(1, cols):
@@ -249,6 +241,17 @@
         copy.start()
 
     packed_in[part] = jnp.zeros((short, LANES), jnp.bfloat16)
+    lax.fori_loop(nodes // depth, counts.shape[0] // depth, tally, 0)
+    for load in loads[6:]:
+        load.wait()
+    mine = (
+        lax.broadcasted_iota(jnp.int32, (width, hid), 0) + column * width
+        == lax.broadcasted_iota(jnp.int32, (width, hid), 1)
+    )
+    mine = jnp.where(mine, 1.0, 0.0).astype(jnp.bfloat16)
+    self_rows = dot(mine, selfw[...], 1, 1).astype(jnp.bfloat16)
+    neigh_rows = dot(mine, neighw[...], 1, 1).astype(jnp.bfloat16)
+
     local_sum = dot(hidden, counts[0:nodes, :], 1, 0)
 
     def arrive(step, carry):

time: 22.3 us -> 22.3 us (level)
  no operation moved by 1% of the time
where the time goes in v3:
time: 22.3 us; the launch traced here: 22.1 us
  Pallas kernels  20.6 us (92%)
  local copies, waits for them, and re-layouts  1.47 us (7%)
    pallas_call x1, Pallas kernels, local(): pl.pallas_call(functools.partial(kernel, cols, parts, capacity), out_shap...  20.6 us
    unnamed x1, local copies, waits for them, and re-layouts  1.47 us

profile of v3, /device:TPU:0, one launch (start us, length us, event | category | flops | bytes accessed | tf_op | source)
XLA Modules:
  0.0 22.1 jit_solution(2638683402682550829)
XLA Ops:
  0.0 20.6 %layer.1 = bf16[64,512]{1,0:T(8,128)(2,1)} custom-call(bf16[192,512]{1,0:T(8,128)(2,1)} %feat_hbm.1, bf16[192,256]{1,0:T(8,128)(2,1)} %proj_hbm.1, bf16[256,256]{1,0:T(8,128)(2,1)} %selfw_hbm.1, bf16[256,256]{1,0:T(8,128)(2,1)} %neighw_hbm.1, s32[16,512]{1,0:T(8,128)} %neigh_hbm.1, s32[1,512]{1,0:T(1,128)} %bitcast.1, s32[1,512]{1,0:T(1,128)} %rows_hbm.1, ...), custom_call_target="tpu_custom_call" | custom-call | tf_op jit(solution)/shard_map/layer/pallas_call | solution.py:326
  20.6 1.5 %copy.10 = bf16[64,512]{1,0:T(8,128)(2,1)} copy(bf16[64,512]{1,0:T(8,128)(2,1)} %layer.1) | data formatting | bytes 131072

commit v4 on v3

--- a/solution.py
+++ b/solution.py
@@ -43,7 +43,6 @@
     outgoing_sum,
     incoming_sum,
     hidden_all,
-    mean_all,
     pick,
     packed_out,
     packed_in,
@@ -56,8 +55,8 @@
     row_recv,
     hid_send,
     hid_recv,
-    mean_send,
-    mean_recv,
+    pass_send,
+    pass_recv,
 ):
     column = lax.axis_index("cols")
     part = lax.axis_index("dom")
@@ -217,7 +216,7 @@
         peer = (part + step) % parts
         return pltpu.make_async_remote_copy(
             src_ref=packed_out.at[peer],
-            dst_ref=packed_in.at[part],
+            dst_ref=packed_in.at[column, part],
             send_sem=row_send.at[step],
             recv_sem=row_recv.at[step],
             device_id=(column, peer),
@@ -240,7 +239,8 @@
     for copy in hidden_copies:
         copy.start()
 
-    packed_in[part] = jnp.zeros((short, LANES), jnp.bfloat16)
+    for index in range(cols):
+        packed_in[index, part] = jnp.zeros((short, LANES), jnp.bfloat16)
     lax.fori_loop(nodes // depth, counts.shape[0] // depth, tally, 0)
     for load in loads[6:]:
         load.wait()
@@ -252,49 +252,63 @@
     self_rows = dot(mine, selfw[...], 1, 1).astype(jnp.bfloat16)
     neigh_rows = dot(mine, neighw[...], 1, 1).astype(jnp.bfloat16)
 
-    local_sum = dot(hidden, counts[0:nodes, :], 1, 0)
+    def forward(step, source):
+        return to_column(
+            packed_in.at[column, source],
+            packed_in.at[column, source],
+            pass_send.at[source],
+            pass_recv.at[source],
+            step,
+        )
 
     def arrive(step, carry):
         to_part(step).wait_recv()
+        for hop in range(1, cols):
+            forward(hop, (part - step + parts) % parts).start()
         return carry
 
     lax.fori_loop(1, parts, arrive, 0)
-
-    half = lax.broadcasted_iota(jnp.int32, (short, LANES), 1) // capacity
-
-    def unpack(index, carry):
-        for piece in range(fold):
-            value = jnp.zeros((short, LANES), jnp.float32)
-            for place in range(fold):
-                block = packed_in[index * fold + place].astype(jnp.float32)
-                shift = (place - piece) * capacity % LANES
-                if shift:
-                    block = pltpu.roll(block, shift, 1)
-                value = jnp.where(half == place, block, value)
-            table[piece * short : (piece + 1) * short, pl.ds(pl.multiple_of(index * LANES, LANES), LANES)] = (
-                value.astype(jnp.bfloat16)
-            )
-        return carry
-
-    lax.fori_loop(0, parts // fold, unpack, 0)
-    summed = local_sum + dot(table[...], counts[nodes:, :], 1, 0)
-    mean_all[band(column), :] = (summed / degree[...].astype(jnp.float32)).astype(jnp.bfloat16)
-    mean_copies = share(mean_all, mean_send, mean_recv)
-    for copy in mean_copies:
-        copy.start()
     for copy in hidden_copies:
         copy.wait_recv()
-    result = dot(self_rows, hidden_all[...], 1, 0)
-    for copy in mean_copies:
-        copy.wait_recv()
-    result = result + dot(neigh_rows, mean_all[...], 1, 0)
+    own[...] = dot(hidden_all[...], counts[0:nodes, :], 1, 0)
+
+    def passed(step, carry):
+        for hop in range(1, cols):
+            forward(hop, (part - step + parts) % parts).wait_recv()
+        return carry
+
+    lax.fori_loop(1, parts, passed, 0)
+
+    half = lax.broadcasted_iota(jnp.int32, (short, LANES), 1) // capacity
+
+    def unpack(index, carry):
+        columns = pl.ds(pl.multiple_of(index * LANES, LANES), LANES)
+        for source in range(cols):
+            for piece in range(fold):
+                value = jnp.zeros((short, LANES), jnp.float32)
+                for place in range(fold):
+                    block = packed_in[source, index * fold + place].astype(jnp.float32)
+                    shift = (place - piece) * capacity % LANES
+                    if shift:
+                        block = pltpu.roll(block, shift, 1)
+                    value = jnp.where(half == place, block, value)
+                start = source * width + piece * short
+                table[start : start + short, columns] = value.astype(jnp.bfloat16)
+        return carry
+
+    lax.fori_loop(0, parts // fold, unpack, 0)
+    summed = own[...] + dot(table[...], counts[nodes:, :], 1, 0)
+    mean = (summed / degree[...].astype(jnp.float32)).astype(jnp.bfloat16)
+    result = dot(self_rows, hidden_all[...], 1, 0) + dot(neigh_rows, mean, 1, 0)
     out_ref[...] = jnp.maximum(result, 0.0).astype(out_ref.dtype)
 
-    for copy in sums + hidden_copies + mean_copies:
+    for copy in sums + hidden_copies:
         copy.wait_send()
 
     def sent(step, carry):
         to_part(step).wait_send()
+        for hop in range(1, cols):
+            forward(hop, (part - step + parts) % parts).wait_send()
         return carry
 
     lax.fori_loop(1, parts, sent, 0)
@@ -334,11 +348,10 @@
             pltpu.VMEM((hid, nodes), bf16),
             pltpu.VMEM((cols - 1, width, nodes), bf16),
             pltpu.VMEM((hid, nodes), bf16),
-            pltpu.VMEM((hid, nodes), bf16),
             pltpu.VMEM((nodes, slots * fold), bf16),
             pltpu.VMEM((parts, short, LANES), bf16),
-            pltpu.VMEM((parts, short, LANES), bf16),
-            pltpu.VMEM((width, slots), bf16),
+            pltpu.VMEM((cols, parts, short, LANES), bf16),
+            pltpu.VMEM((hid, slots), bf16),
             pltpu.VMEM((nodes + slots, nodes), bf16),
             copies((len(arguments),)),
             copies((cols - 1,)),
@@ -347,8 +360,8 @@
             copies((parts,)),
             copies((cols - 1,)),
             copies((cols - 1,)),
-            copies((cols - 1,)),
-            copies((cols - 1,)),
+            copies((parts, cols - 1)),
+            copies((parts, cols - 1)),
         ],
         compiler_params=pltpu.CompilerParams(
             collective_id=0, has_side_effects=True, vmem_limit_bytes=67043328

time: 22.3 us -> 22.4 us (level)
  no operation moved by 1% of the time
where the time goes in v4:
time: 22.4 us; the launch traced here: 22.2 us
  Pallas kernels  20.7 us (92%)
  local copies, waits for them, and re-layouts  1.47 us (7%)
    pallas_call x1, Pallas kernels, local(): pl.pallas_call(functools.partial(kernel, cols, parts, capacity), out_shap...  20.7 us
    unnamed x1, local copies, waits for them, and re-layouts  1.47 us

profile of v4, /device:TPU:0, one launch (start us, length us, event | category | flops | bytes accessed | tf_op | source)
XLA Modules:
  0.0 22.2 jit_solution(14574033466867999868)
XLA Ops:
  0.0 20.7 %layer.1 = bf16[64,512]{1,0:T(8,128)(2,1)} custom-call(bf16[192,512]{1,0:T(8,128)(2,1)} %feat_hbm.1, bf16[192,256]{1,0:T(8,128)(2,1)} %proj_hbm.1, bf16[256,256]{1,0:T(8,128)(2,1)} %selfw_hbm.1, bf16[256,256]{1,0:T(8,128)(2,1)} %neighw_hbm.1, s32[16,512]{1,0:T(8,128)} %neigh_hbm.1, s32[1,512]{1,0:T(1,128)} %bitcast.1, s32[1,512]{1,0:T(1,128)} %rows_hbm.1, ...), custom_call_target="tpu_custom_call" | custom-call | tf_op jit(solution)/shard_map/layer/pallas_call | solution.py:340
  20.7 1.5 %copy.10 = bf16[64,512]{1,0:T(8,128)(2,1)} copy(bf16[64,512]{1,0:T(8,128)(2,1)} %layer.1) | data formatting | bytes 131072
